TPU v7x, 32 devices: a whole 2x2x4 slice. The times are simulated.
32 devices in a mesh: row: 8 (over y, x, core), col: 4 (over z).
Axes of the slice: x: 2, y: 2, z: 4, core: 2. Of those that a mesh axis runs over, the one named last changes fastest.
Arguments:
- pair: bfloat16 [256, 256, 128], P('row', 'col'), may hold values from -6 to 6
- group: bfloat16 [32, 256, 128], P('col', 'row'), may hold values from -6 to 6
- w_query: bfloat16 [128, 128], replicated, may hold values from -0.5 to 0.5
- w_key: bfloat16 [128, 128], replicated, may hold values from -0.5 to 0.5
- w_value: bfloat16 [128, 128], replicated, may hold values from -0.5 to 0.5
- w_gate: bfloat16 [128, 128], replicated, may hold values from -0.5 to 0.5
- w_bias: float32 [128, 4], replicated, may hold values from -40 to 40
- w_out: bfloat16 [128, 128], replicated, may hold values from -0.5 to 0.5
Outputs:
- update: bfloat16 [32, 256, 128], P('col', 'row')
All inputs are finite; a program needn't handle non-finite values.
Results may differ from a plain program's by a relative error of at most 0.012.
Values may be sent and summed in bfloat16 or wider, within the bound.
No kernel may reach another device: no remote copies, remote signals or barrier semaphores. Data moves between devices by JAX's collectives and lax.ppermute only.
A program may use at most 64 MiB of HBM per device.

v0:
```python
import math
import jax
import jax.numpy as jnp
from jax import lax
from jax.sharding import PartitionSpec as P

EPS = 1e-05


def normalize(entries):
    average = jnp.mean(entries, axis=-1, keepdims=True)
    centered = entries - average
    spread = jnp.mean(centered * centered, axis=-1, keepdims=True)
    return centered * lax.rsqrt(spread + EPS)


def per_device(pair, group, w_query, w_key, w_value, w_gate, w_bias, w_out):
    head_count = w_bias.shape[1]
    proj_width = w_query.shape[1]
    head_dim = proj_width // head_count
    query_rows, pair_cols, channels = group.shape
    normed_pair = normalize(pair.astype(jnp.float32))
    bias_local = jnp.einsum("jkc,ch->hjk", normed_pair, w_bias, precision=lax.Precision.HIGHEST)
    bias_panel = lax.all_gather(bias_local, "col", axis=2, tiled=True)
    normed = normalize(group.astype(jnp.float32)).astype(jnp.bfloat16)
    flat_rows = normed.reshape(-1, channels)
    scale = 1.0 / math.sqrt(head_dim)
    query = (jnp.dot(flat_rows, w_query, preferred_element_type=jnp.float32) * scale).astype(
        jnp.bfloat16
    )
    query = query.reshape(query_rows, pair_cols, head_count, head_dim)
    gating = jax.nn.sigmoid(jnp.dot(flat_rows, w_gate, preferred_element_type=jnp.float32))
    gating = gating.reshape(query_rows, pair_cols, head_count, head_dim)
    block_rows = lax.all_gather(normed, "row", axis=1, tiled=True)
    key_count = block_rows.shape[1]
    block_flat = block_rows.reshape(-1, channels)
    key_part = jnp.dot(block_flat, w_key, preferred_element_type=jnp.float32).astype(jnp.bfloat16)
    value_part = jnp.dot(block_flat, w_value, preferred_element_type=jnp.float32).astype(
        jnp.bfloat16
    )
    key_part = key_part.reshape(query_rows, key_count, head_count, head_dim)
    value_part = value_part.reshape(query_rows, key_count, head_count, head_dim)
    run_max = jnp.full((query_rows, head_count, pair_cols), -1e30, jnp.float32)
    scores = (
        jnp.einsum("ijhd,ikhd->ihjk", query, key_part, preferred_element_type=jnp.float32)
        + bias_panel[None]
    )
    new_max = jnp.maximum(run_max, jnp.max(scores, axis=-1))
    weights = jnp.exp(scores - new_max[..., None])
    run_sum = jnp.sum(weights, axis=-1)
    mixture = jnp.einsum(
        "ihjk,ikhd->ijhd",
        weights.astype(jnp.bfloat16),
        value_part,
        preferred_element_type=jnp.float32,
    )
    accumulated = mixture
    run_max, run_sum, accumulated = (new_max, run_sum, accumulated)
    attention = accumulated / jnp.transpose(run_sum, (0, 2, 1))[..., None]
    hidden = (gating * attention).astype(jnp.bfloat16).reshape(-1, proj_width)
    result = jnp.dot(hidden, w_out, preferred_element_type=jnp.float32).astype(jnp.bfloat16)
    return result.reshape(query_rows, pair_cols, channels)


def solution(mesh):
    in_specs = (P("row", "col", None), P("col", "row", None), P(), P(), P(), P(), P(), P())
    out_specs = P("col", "row", None)
    return jax.shard_map(
        per_device, mesh=mesh, in_specs=in_specs, out_specs=out_specs, check_vma=False
    )
```

profile of v0, /device:TPU:0, one launch (start us, length us, event | category | flops | bytes accessed | tf_op | source)
XLA Modules:
  0.0 40.9 jit_solution(7191558274230785309)
XLA Ops:
  0.0 0.0 copy-start
  0.0 0.0 copy-start.2
  0.0 1.0 %convert_reduce_fusion.1 = f32[8,32]{1,0:T(8,128)S(1)} fusion(bf16[8,32,128]{2,1,0:T(8,128)(2,1)} %param.9), kind=kLoop, calls=%fused_computation.30 | loop fusion | flops 65280 | bytes 66560 | tf_op jit(solution)/shard_map/reduce_sum | solution.py:11
  1.0 0.0 copy-done.2
  1.0 0.2 fusion.22
  1.2 0.1 fusion.23
  1.4 11.3 %all_gather.6 = bf16[8,256,128]{2,1,0:T(8,128)(2,1)S(1)} all-gather(bf16[8,32,128]{2,1,0:T(8,128)(2,1)S(1)} %fusion.23), channel_id=1, replica_groups=mesh['row'=8,'col'=4] {'row'}, dimensions={1}, use_global_device_ids=true | all-gather | bytes 589824 | tf_op jit(solution)/shard_map/all_gather | solution.py:34
  12.7 0.0 copy-done
  12.7 0.3 convolution_convert_fusion
  13.0 0.2 copy.23
  13.2 0.0 copy-start.3
  13.2 0.0 copy-start.1
  13.3 0.1 copy.32
  13.4 0.6 %copy-done.3 = bf16[128,128]{1,0:T(8,128)(2,1)S(1)} copy-done((bf16[128,128]{1,0:T(8,128)(2,1)S(1)}, bf16[128,128]{1,0:T(8,128)(2,1)}, u32[]{:S(2)}) %copy-start.3) | copy-done | bytes 32792
  14.0 0.1 fusion.8
  14.1 0.2 reshape.57
  14.3 0.0 copy-done.1
  14.3 0.3 convert_reduce_fusion
  14.7 0.6 %fusion.9 = f32[32,64]{1,0:T(8,128)S(1)} fusion(bf16[32,64,128]{2,1,0:T(8,128)(2,1)S(1)} %copy-done.1, f32[32,64]{1,0:T(8,128)S(1)} %broadcast_multiply_fusion), kind=kLoop, calls=%fused_computation.19 | loop fusion | flops 1046528 | bytes 540672 | tf_op jit(solution)/shard_map/reduce_sum | solution.py:13
  15.3 0.0 copy-start.7
  15.4 0.7 %copy-done.7 = f32[128,4]{0,1:T(4,128)S(1)} copy-done((f32[128,4]{0,1:T(4,128)S(1)}, f32[128,4]{0,1:T(4,128)}, u32[]{:S(2)}) %copy-start.7) | copy-done | bytes 2072
  16.0 2.9 %convolution_bitcast_fusion.1 = f32[4,32,64]{2,0,1:T(4,128)S(1)} fusion(bf16[32,64,128]{2,1,0:T(8,128)(2,1)S(1)} %copy-done.1, f32[32,64]{1,0:T(8,128)S(1)} %add_rsqrt_fusion, f32[32,64]{1,0:T(8,128)S(1)} %broadcast_multiply_fusion, f32[128,4]{0,1:T(4,128)S(1)} %copy-done.7), kind=kOutput, calls=%fused_computation.18 | convolution fusion | flops 13369344 | bytes 575488 | tf_op jit(solution)/shard_map/jkc,ch->hjk/dot_general | solution.py:23
  18.9 0.1 copy.26
  19.1 16.3 %all_gather.7 = f32[4,32,256]{1,0,2:T(4,128)S(1)} all-gather(f32[4,32,64]{1,0,2:T(4,128)S(1)} %copy.26), channel_id=1, replica_groups=mesh['row'=8,'col'=4] {'col'}, dimensions={2}, use_global_device_ids=true | all-gather | bytes 163840 | tf_op jit(solution)/shard_map/all_gather | solution.py:24
  35.4 0.2 copy.27
  35.6 0.4 fusion.25
  36.0 0.0 copy-start.4
  36.0 0.4 %fusion.11 = f32[8,4,32]{2,1,0:T(4,128)S(1)} fusion(f32[8,4,32,256]{3,2,1,0:T(8,128)S(1)} %get-tuple-element.6, f32[8,4,32]{2,1,0:T(4,128)S(1)} %broadcast_maximum_fusion), kind=kLoop, calls=%fused_computation.21 | loop fusion | flops 523264 | bytes 1056768 | tf_op jit(solution)/shard_map/reduce_sum | solution.py:50
  36.4 0.3 copy-done.4
  36.8 0.3 convolution_convert_fusion.1
  37.0 0.2 copy.22
  37.3 0.0 copy-start.6
  37.3 0.1 copy.31
  37.4 0.6 %copy-done.6 = bf16[128,128]{1,0:T(8,128)(2,1)S(1)} copy-done((bf16[128,128]{1,0:T(8,128)(2,1)S(1)}, bf16[128,128]{1,0:T(8,128)(2,1)}, u32[]{:S(2)}) %copy-start.6) | copy-done | bytes 32792
  38.0 0.2 fusion.7
  38.2 0.3 reshape.54
  38.5 0.2 copy.29
  38.7 0.4 fusion.4
  39.1 0.2 copy.30
  39.3 0.0 copy-start.5
  39.3 0.2 reshape.59
  39.5 0.6 %copy-done.5 = bf16[128,128]{1,0:T(8,128)(2,1)S(1)} copy-done((bf16[128,128]{1,0:T(8,128)(2,1)S(1)}, bf16[128,128]{1,0:T(8,128)(2,1)}, u32[]{:S(2)}) %copy-start.5) | copy-done | bytes 32792
  40.0 0.8 %convolution_convert_fusion.2 = bf16[256,128]{1,0:T(8,128)(2,1)} fusion(bf16[256,128]{0,1:T(8,128)(2,1)S(1)} %reshape.59, bf16[128,128]{1,0:T(8,128)(2,1)S(1)} %copy-done.5), kind=kOutput, calls=%fused_computation.16 | convolution fusion | flops 8421376 | bytes 163840 | tf_op jit(solution)/shard_map/dot_general | solution.py:61
  (5 shorter events, 0.0 us)
Async XLA Ops:
  0.0 12.7 %copy-start = (bf16[128,128]{1,0:T(8,128)(2,1)S(1)}, bf16[128,128]{1,0:T(8,128)(2,1)}, u32[]{:S(2)}) copy-start(bf16[128,128]{1,0:T(8,128)(2,1)} %param.11) | copy-start | bytes 98308
  0.0 1.0 %copy-start.2 = (bf16[8,32,128]{2,1,0:T(8,128)(2,1)S(1)}, bf16[8,32,128]{2,1,0:T(8,128)(2,1)}, u32[]{:S(2)}) copy-start(bf16[8,32,128]{2,1,0:T(8,128)(2,1)} %param.9) | copy-start | bytes 196612
  13.2 0.8 %copy-start.3 = (bf16[128,128]{1,0:T(8,128)(2,1)S(1)}, bf16[128,128]{1,0:T(8,128)(2,1)}, u32[]{:S(2)}) copy-start(bf16[128,128]{1,0:T(8,128)(2,1)} %param.10) | copy-start | bytes 98308
  13.2 1.1 %copy-start.1 = (bf16[32,64,128]{2,1,0:T(8,128)(2,1)S(1)}, bf16[32,64,128]{2,1,0:T(8,128)(2,1)}, u32[]{:S(2)}) copy-start(bf16[32,64,128]{2,1,0:T(8,128)(2,1)} %param.8) | copy-start | bytes 1572868
  15.3 0.7 %copy-start.7 = (f32[128,4]{0,1:T(4,128)S(1)}, f32[128,4]{0,1:T(4,128)}, u32[]{:S(2)}) copy-start(f32[128,4]{0,1:T(4,128)} %param.14) | copy-start | bytes 6148
  36.0 0.8 %copy-start.4 = (bf16[128,128]{1,0:T(8,128)(2,1)S(1)}, bf16[128,128]{1,0:T(8,128)(2,1)}, u32[]{:S(2)}) copy-start(bf16[128,128]{1,0:T(8,128)(2,1)} %param.12) | copy-start | bytes 98308
  37.3 0.8 %copy-start.6 = (bf16[128,128]{1,0:T(8,128)(2,1)S(1)}, bf16[128,128]{1,0:T(8,128)(2,1)}, u32[]{:S(2)}) copy-start(bf16[128,128]{1,0:T(8,128)(2,1)} %param.13) | copy-start | bytes 98308
  39.3 0.8 %copy-start.5 = (bf16[128,128]{1,0:T(8,128)(2,1)S(1)}, bf16[128,128]{1,0:T(8,128)(2,1)}, u32[]{:S(2)}) copy-start(bf16[128,128]{1,0:T(8,128)(2,1)} %param.15) | copy-start | bytes 98308
where the time goes:
time: 41.3 us; the launch traced here: 40.9 us
  blocking collectives  27.7 us (67%)
  matrix products  5.42 us (13%)
  local copies, waits for them, and re-layouts  4.77 us (12%)
  other arithmetic  2.76 us (7%)
    all_gather x1, blocking collectives, per_device(): bias_panel = lax.all_gather(bias_local, 'col', axis=2, tiled=True)  16.3 us
    all_gather x1, blocking collectives, per_device(): block_rows = lax.all_gather(normed, 'row', axis=1, tiled=True)  11.3 us
    unnamed x18, local copies, waits for them, and re-layouts  3.06 us
    dot_general x1, matrix products, per_device(): jnp.einsum('jkc,ch->hjk', normed_pair, w_bias, precision=lax.Precision.HI...  2.93 us
    reduce_sum x2, other arithmetic, normalize(): average = jnp.mean(entries, axis=-1, keepdims=True)  1.35 us

commit v1 on v0

--- a/solution.py
+++ b/solution.py
@@ -21,7 +21,8 @@
     query_rows, pair_cols, channels = group.shape
     normed_pair = normalize(pair.astype(jnp.float32))
     bias_local = jnp.einsum("jkc,ch->hjk", normed_pair, w_bias, precision=lax.Precision.HIGHEST)
-    bias_panel = lax.all_gather(bias_local, "col", axis=2, tiled=True)
+    pieces = lax.all_gather(bias_local, "col", axis=0, tiled=False)
+    bias_panel = jnp.concatenate(pieces, axis=2)
     normed = normalize(group.astype(jnp.float32)).astype(jnp.bfloat16)
     flat_rows = normed.reshape(-1, channels)
     scale = 1.0 / math.sqrt(head_dim)

time: 41.3 us -> 39.1 us (0.947)
  blocking collectives: 27.7 us -> 25.4 us
    all_gather x1, blocking collectives: 16.3 us -> 14.1 us  [per_device(): pieces = lax.all_gather(bias_local, 'col', axis=0, tiled=False)]
where the time goes in v1:
time: 39.1 us; the launch traced here: 38.7 us
  blocking collectives  25.4 us (65%)
  matrix products  5.43 us (14%)
  local copies, waits for them, and re-layouts  4.85 us (12%)
  other arithmetic  2.76 us (7%)
    all_gather x1, blocking collectives, per_device(): pieces = lax.all_gather(bias_local, 'col', axis=0, tiled=False)  14.1 us
    all_gather x1, blocking collectives, per_device(): block_rows = lax.all_gather(normed, 'row', axis=1, tiled=True)  11.3 us
    unnamed x18, local copies, waits for them, and re-layouts  3.06 us
    dot_general x1, matrix products, per_device(): jnp.einsum('jkc,ch->hjk', normed_pair, w_bias, precision=lax.Precision.HI...  2.93 us
    reduce_sum x2, other arithmetic, normalize(): average = jnp.mean(entries, axis=-1, keepdims=True)  1.35 us
    dot_general x1, matrix products, per_device(): jnp.dot(hidden, w_out, preferred_element_type=jnp.float32)  0.82 us
    reduce_sum x2, other arithmetic, normalize(): spread = jnp.mean(centered * centered, axis=-1, keepdims=True)  0.82 us

profile of v1, /device:TPU:0, one launch (start us, length us, event | category | flops | bytes accessed | tf_op | source)
XLA Modules:
  0.0 38.7 jit_solution(10114434642766362012)
XLA Ops:
  0.0 0.0 copy-start
  0.0 0.0 copy-start.2
  0.0 1.0 %convert_reduce_fusion.1 = f32[8,32]{1,0:T(8,128)S(1)} fusion(bf16[8,32,128]{2,1,0:T(8,128)(2,1)} %param.9), kind=kLoop, calls=%fused_computation.30 | loop fusion | flops 65280 | bytes 66560 | tf_op jit(solution)/shard_map/reduce_sum | solution.py:11
  1.0 0.0 copy-done.2
  1.0 0.2 fusion.22
  1.2 0.1 fusion.23
  1.4 11.3 %all_gather.9 = bf16[8,256,128]{2,1,0:T(8,128)(2,1)S(1)} all-gather(bf16[8,32,128]{2,1,0:T(8,128)(2,1)S(1)} %fusion.23), channel_id=1, replica_groups=mesh['row'=8,'col'=4] {'row'}, dimensions={1}, use_global_device_ids=true | all-gather | bytes 589824 | tf_op jit(solution)/shard_map/all_gather | solution.py:35
  12.7 0.0 copy-done
  12.7 0.3 convolution_convert_fusion
  13.0 0.2 copy.23
  13.2 0.0 copy-start.3
  13.2 0.0 copy-start.1
  13.3 0.1 copy.32
  13.4 0.6 %copy-done.3 = bf16[128,128]{1,0:T(8,128)(2,1)S(1)} copy-done((bf16[128,128]{1,0:T(8,128)(2,1)S(1)}, bf16[128,128]{1,0:T(8,128)(2,1)}, u32[]{:S(2)}) %copy-start.3) | copy-done | bytes 32792
  14.0 0.1 fusion.8
  14.1 0.2 reshape.60
  14.3 0.0 copy-done.1
  14.3 0.3 convert_reduce_fusion
  14.7 0.6 %fusion.9 = f32[32,64]{1,0:T(8,128)S(1)} fusion(bf16[32,64,128]{2,1,0:T(8,128)(2,1)S(1)} %copy-done.1, f32[32,64]{1,0:T(8,128)S(1)} %broadcast_multiply_fusion), kind=kLoop, calls=%fused_computation.19 | loop fusion | flops 1046528 | bytes 540672 | tf_op jit(solution)/shard_map/reduce_sum | solution.py:13
  15.3 0.0 copy-start.7
  15.4 0.7 %copy-done.7 = f32[128,4]{0,1:T(4,128)S(1)} copy-done((f32[128,4]{0,1:T(4,128)S(1)}, f32[128,4]{0,1:T(4,128)}, u32[]{:S(2)}) %copy-start.7) | copy-done | bytes 2072
  16.0 2.9 %convolution_bitcast_fusion.1 = f32[4,32,64]{2,0,1:T(4,128)S(1)} fusion(bf16[32,64,128]{2,1,0:T(8,128)(2,1)S(1)} %copy-done.1, f32[32,64]{1,0:T(8,128)S(1)} %add_rsqrt_fusion, f32[32,64]{1,0:T(8,128)S(1)} %broadcast_multiply_fusion, f32[128,4]{0,1:T(4,128)S(1)} %copy-done.7), kind=kOutput, calls=%fused_computation.18 | convolution fusion | flops 13369344 | bytes 575488 | tf_op jit(solution)/shard_map/jkc,ch->hjk/dot_general | solution.py:23
  19.0 14.1 %all-gather = f32[16,32,64]{2,1,0:T(8,128)S(1)} all-gather(f32[4,32,64]{2,1,0:T(8,128)S(1)} %copy.26), channel_id=2, replica_groups=mesh['row'=8,'col'=4] {'col'}, dimensions={0}, use_global_device_ids=true | all-gather | bytes 163840 | tf_op jit(solution)/shard_map/all_gather | solution.py:24
  33.1 0.2 copy.27
  33.2 0.2 add.40
  33.4 0.4 %fusion.25 = (f32[8,4,32]{2,1,0:T(4,128)S(1)}, f32[8,4,32,256]{3,2,1,0:T(8,128)S(1)}) fusion(f32[4,32,256]{2,1,0:T(8,128)S(1)} %add.40, bf16[8,256,4,32]{1,0,3,2:T(8,128)(2,1)S(1)} %bitcast.48, bf16[8,32,4,32]{3,2,1,0:T(4,128)(2,1)S(1)} %reshape.60), kind=kOutput, calls=%fused_computation.41 | convolution fusion | flops 17300480 | bytes 1773568 | tf_op jit(solution)/shard_map/ijhd,ikhd->ihjk/dot_general | solution.py:46
  33.9 0.0 copy-start.4
  33.9 0.4 %fusion.11 = f32[8,4,32]{2,1,0:T(4,128)S(1)} fusion(f32[8,4,32,256]{3,2,1,0:T(8,128)S(1)} %get-tuple-element.6, f32[8,4,32]{2,1,0:T(4,128)S(1)} %broadcast_maximum_fusion), kind=kLoop, calls=%fused_computation.21 | loop fusion | flops 523264 | bytes 1056768 | tf_op jit(solution)/shard_map/reduce_sum | solution.py:51
  34.3 0.3 copy-done.4
  34.6 0.3 convolution_convert_fusion.1
  34.9 0.2 copy.22
  35.1 0.0 copy-start.6
  35.1 0.1 copy.31
  35.2 0.6 %copy-done.6 = bf16[128,128]{1,0:T(8,128)(2,1)S(1)} copy-done((bf16[128,128]{1,0:T(8,128)(2,1)S(1)}, bf16[128,128]{1,0:T(8,128)(2,1)}, u32[]{:S(2)}) %copy-start.6) | copy-done | bytes 32792
  35.9 0.2 fusion.7
  36.1 0.3 reshape.57
  36.3 0.2 copy.29
  36.5 0.4 %fusion.4 = bf16[8,32,4,32]{1,3,2,0:T(8,128)(2,1)S(1)} fusion(f32[8,32,4,32]{1,3,2,0:T(8,128)S(1)} %copy.29, f32[8,4,32,256]{3,2,1,0:T(8,128)S(1)} %get-tuple-element.6, bf16[8,256,4,32]{1,0,3,2:T(8,128)(2,1)S(1)} %bitcast.52, f32[8,4,32]{2,1,0:T(4,128)S(1)} %broadcast_maximum_fusion, f32[8,32,4]{1,2,0:T(4,128)S(1)} %bitcast.53), kind=kOutput, calls=%fused_computation.10 | convolution fusion | flops 17399808 | bytes 1777664 | tf_op jit(solution)/shard_map/ihjk,ikhd->ijhd/dot_general | solution.py:52
  36.9 0.2 copy.30
  37.1 0.0 copy-start.5
  37.1 0.2 reshape.63
  37.3 0.6 %copy-done.5 = bf16[128,128]{1,0:T(8,128)(2,1)S(1)} copy-done((bf16[128,128]{1,0:T(8,128)(2,1)S(1)}, bf16[128,128]{1,0:T(8,128)(2,1)}, u32[]{:S(2)}) %copy-start.5) | copy-done | bytes 32792
  37.9 0.8 %convolution_convert_fusion.2 = bf16[256,128]{1,0:T(8,128)(2,1)} fusion(bf16[256,128]{0,1:T(8,128)(2,1)S(1)} %reshape.63, bf16[128,128]{1,0:T(8,128)(2,1)S(1)} %copy-done.5), kind=kOutput, calls=%fused_computation.16 | convolution fusion | flops 8421376 | bytes 163840 | tf_op jit(solution)/shard_map/dot_general | solution.py:62
  (6 shorter events, 0.0 us)
Async XLA Ops:
  0.0 12.7 %copy-start = (bf16[128,128]{1,0:T(8,128)(2,1)S(1)}, bf16[128,128]{1,0:T(8,128)(2,1)}, u32[]{:S(2)}) copy-start(bf16[128,128]{1,0:T(8,128)(2,1)} %param.11) | copy-start | bytes 98308
  0.0 1.0 %copy-start.2 = (bf16[8,32,128]{2,1,0:T(8,128)(2,1)S(1)}, bf16[8,32,128]{2,1,0:T(8,128)(2,1)}, u32[]{:S(2)}) copy-start(bf16[8,32,128]{2,1,0:T(8,128)(2,1)} %param.9) | copy-start | bytes 196612
  13.2 0.8 %copy-start.3 = (bf16[128,128]{1,0:T(8,128)(2,1)S(1)}, bf16[128,128]{1,0:T(8,128)(2,1)}, u32[]{:S(2)}) copy-start(bf16[128,128]{1,0:T(8,128)(2,1)} %param.10) | copy-start | bytes 98308
  13.2 1.1 %copy-start.1 = (bf16[32,64,128]{2,1,0:T(8,128)(2,1)S(1)}, bf16[32,64,128]{2,1,0:T(8,128)(2,1)}, u32[]{:S(2)}) copy-start(bf16[32,64,128]{2,1,0:T(8,128)(2,1)} %param.8) | copy-start | bytes 1572868
  15.3 0.7 %copy-start.7 = (f32[128,4]{0,1:T(4,128)S(1)}, f32[128,4]{0,1:T(4,128)}, u32[]{:S(2)}) copy-start(f32[128,4]{0,1:T(4,128)} %param.14) | copy-start | bytes 6148
  33.9 0.8 %copy-start.4 = (bf16[128,128]{1,0:T(8,128)(2,1)S(1)}, bf16[128,128]{1,0:T(8,128)(2,1)}, u32[]{:S(2)}) copy-start(bf16[128,128]{1,0:T(8,128)(2,1)} %param.12) | copy-start | bytes 98308
  35.1 0.8 %copy-start.6 = (bf16[128,128]{1,0:T(8,128)(2,1)S(1)}, bf16[128,128]{1,0:T(8,128)(2,1)}, u32[]{:S(2)}) copy-start(bf16[128,128]{1,0:T(8,128)(2,1)} %param.13) | copy-start | bytes 98308
  37.1 0.8 %copy-start.5 = (bf16[128,128]{1,0:T(8,128)(2,1)S(1)}, bf16[128,128]{1,0:T(8,128)(2,1)}, u32[]{:S(2)}) copy-start(bf16[128,128]{1,0:T(8,128)(2,1)} %param.15) | copy-start | bytes 98308
